TPU v7x, 32 devices: a whole 2x2x4 slice. The times are simulated.
32 devices in a mesh: fsdp: 4 (over z), ctx: 2 (over x), tp: 4 (over y, core).
Axes of the slice: x: 2, y: 2, z: 4, core: 2. Of those that a mesh axis runs over, the one named last changes fastest.
Arguments:
- inputs: float32 [4, 2048, 768], P('fsdp', 'ctx'), may hold values from -6 to 6
- lengths: int32 [4], P('fsdp'), may hold values from 1024 to 2048, as said below
- w_qkv: float32 [768, 2304], P(('fsdp', 'ctx'), 'tp'), may hold values from -0.3125 to 0.3125
- b_query: float32 [768], P('tp'), may hold values from -3 to 3
- b_value: float32 [768], P('tp'), may hold values from -0.3 to 0.3
- w_out: float32 [768, 768], P('tp', ('fsdp', 'ctx')), may hold values from -1.75 to 1.75
- b_out: float32 [768], replicated, may hold values from -2 to 2
- gain_attn: float32 [768], replicated, may hold values from 0.5 to 1.5
- shift_attn: float32 [768], replicated, may hold values from -2 to 2
- w_up: float32 [768, 3072], P(('fsdp', 'ctx'), 'tp'), may hold values from -0.21875 to 0.21875
- b_up: float32 [3072], P('tp'), may hold values from -3 to 3
- w_down: float32 [3072, 768], P('tp', ('fsdp', 'ctx')), may hold values from -0.109375 to 0.109375
- b_down: float32 [768], replicated, may hold values from -2 to 2
- gain_ffn: float32 [768], replicated, may hold values from 0.5 to 1.5
- shift_ffn: float32 [768], replicated, may hold values from -2 to 2
- cotangent: float32 [4, 2048, 768], P('fsdp', 'ctx'), may hold values from -6 to 6
Outputs:
- outputs: float32 [4, 2048, 768], P('fsdp', 'ctx')
- d_inputs: float32 [4, 2048, 768], P('fsdp', 'ctx')
- d_wqkv: float32 [768, 2304], P(('fsdp', 'ctx'), 'tp')
- d_bquery: float32 [768], P('tp')
- d_bvalue: float32 [768], P('tp')
- d_wout: float32 [768, 768], P('tp', ('fsdp', 'ctx'))
- d_bout: float32 [768], replicated
- d_gattn: float32 [768], replicated
- d_sattn: float32 [768], replicated
- d_wup: float32 [768, 3072], P(('fsdp', 'ctx'), 'tp')
- d_bup: float32 [3072], P('tp')
- d_wdown: float32 [3072, 768], P('tp', ('fsdp', 'ctx'))
- d_bdown: float32 [768], replicated
- d_gffn: float32 [768], replicated
- d_sffn: float32 [768], replicated
Inputs may be any that keep to these rules, and one draw needn't show every extreme that they name: `lengths`: keys at positions at or past a sequence's length are padding; some sequence is full, some has exactly half of 2048 real positions.
All inputs are finite; a program needn't handle non-finite values.
Results may differ from a plain program's by a relative error of at most 0.0003.
Values sent between devices are 32-bit elements; how exact they have to be, the bound alone decides.
A program may use at most 256 MiB of HBM per device.

v0:
```python
import jax
import jax.numpy as jnp
from jax import lax
from jax.sharding import PartitionSpec as P

HD = 64
NORM_EPS = 1e-12
MASKED = -1e30
EXACT = lax.Precision.HIGHEST


def shifted(block, axis, distance):
    devices = range(lax.axis_size(axis))
    route = [((i - distance) % len(devices), i) for i in devices]
    return lax.ppermute(block, axis, route)


def layer_norm(values, gain, shift):
    centred = values - jnp.mean(values, axis=-1, keepdims=True)
    spread = jnp.mean(centred * centred, axis=-1, keepdims=True)
    return centred * lax.rsqrt(spread + NORM_EPS) * gain + shift


def exact_gelu(values):
    return jax.nn.gelu(values, approximate=False)


def per_device(
    inputs,
    lengths,
    w_qkv,
    b_query,
    b_value,
    w_out,
    b_out,
    gain_attn,
    shift_attn,
    w_up,
    b_up,
    w_down,
    b_down,
    gain_ffn,
    shift_ffn,
    cotangent,
):
    model_width = inputs.shape[-1]
    block_len = inputs.shape[1]
    local_heads = b_query.shape[0] // HD
    split_at = local_heads * HD
    inv_root = HD ** (-0.5)
    tokens = inputs.reshape(block_len, model_width)
    length = lengths[0]
    wide_qkv, wide_out, wide_up, wide_down = (
        lax.all_gather(w_qkv, ("fsdp", "ctx"), axis=0, tiled=True),
        lax.all_gather(w_out, ("fsdp", "ctx"), axis=1, tiled=True),
        lax.all_gather(w_up, ("fsdp", "ctx"), axis=0, tiled=True),
        lax.all_gather(w_down, ("fsdp", "ctx"), axis=1, tiled=True),
    )
    bias_qkv = jnp.stack(
        [
            b_query.reshape(local_heads, HD),
            jnp.zeros((local_heads, HD), jnp.float32),
            b_value.reshape(local_heads, HD),
        ],
        axis=1,
    ).reshape(-1)
    projected = (jnp.dot(tokens, wide_qkv, precision=EXACT) + bias_qkv).reshape(
        block_len, local_heads, 3, HD
    )
    head_q = jnp.transpose(projected[:, :, 0], (1, 0, 2))
    kv_pack = jnp.transpose(projected[:, :, 1:], (0, 2, 1, 3)).reshape(block_len, 2 * split_at)

    def unpack(kv_piece):
        key_count = kv_piece.shape[0]
        return (
            kv_piece[:, :split_at].reshape(key_count, local_heads, HD),
            kv_piece[:, split_at:].reshape(key_count, local_heads, HD),
        )

    def key_allowed(key_start, key_count):
        return (key_start + lax.iota(jnp.int32, key_count) < length)[None, None, :]

    kv_piece = lax.all_gather(kv_pack, "ctx", axis=0, tiled=True)
    run_max = jnp.full((local_heads, block_len), MASKED, jnp.float32)
    keys_here, values_here = unpack(kv_piece)
    allowed = key_allowed(jnp.int32(0), kv_piece.shape[0])
    scores = jnp.einsum("hqd,khd->hqk", head_q, keys_here, precision=EXACT) * inv_root
    scores = jnp.where(allowed, scores, MASKED)
    new_max = jnp.maximum(run_max, jnp.max(scores, axis=-1))
    key_probs = jnp.where(allowed, jnp.exp(scores - new_max[..., None]), 0.0)
    run_sum = jnp.sum(key_probs, axis=-1)
    weighted = jnp.einsum("hqk,khd->hqd", key_probs, values_here, precision=EXACT)
    run_max, run_sum, weighted = (new_max, run_sum, weighted)
    head_out = weighted / run_sum[..., None]
    log_sums = run_max + jnp.log(run_sum)
    attended = jnp.transpose(head_out, (1, 0, 2)).reshape(block_len, split_at)
    attn_resid = tokens + lax.psum(jnp.dot(attended, wide_out, precision=EXACT), "tp") + b_out
    attn_normed, first_back = jax.vjp(layer_norm, attn_resid, gain_attn, shift_attn)
    hidden_pre = jnp.dot(attn_normed, wide_up, precision=EXACT) + b_up
    activated, gelu_back = jax.vjp(exact_gelu, hidden_pre)
    ffn_resid = (
        attn_normed + lax.psum(jnp.dot(activated, wide_down, precision=EXACT), "tp") + b_down
    )
    outputs, second_back = jax.vjp(layer_norm, ffn_resid, gain_ffn, shift_ffn)
    grad_second, d_gffn, d_sffn = second_back(cotangent.reshape(block_len, model_width))
    d_wdown = jnp.dot(activated.T, grad_second, precision=EXACT)
    d_bdown = jnp.sum(grad_second, axis=0)
    (grad_pre,) = gelu_back(jnp.dot(grad_second, wide_down.T, precision=EXACT))
    d_wup = jnp.dot(attn_normed.T, grad_pre, precision=EXACT)
    d_bup = jnp.sum(grad_pre, axis=0)
    grad_first = grad_second + lax.psum(jnp.dot(grad_pre, wide_up.T, precision=EXACT), "tp")
    grad_mid, d_gattn, d_sattn = first_back(grad_first)
    d_wout = jnp.dot(attended.T, grad_mid, precision=EXACT)
    d_bout = jnp.sum(grad_mid, axis=0)
    grad_heads = jnp.transpose(
        jnp.dot(grad_mid, wide_out.T, precision=EXACT).reshape(block_len, local_heads, HD),
        (1, 0, 2),
    )
    deltas = jnp.sum(grad_heads * head_out, axis=-1)

    def key_grads(grad_q, kv_piece, key_start):
        keys_here, values_here = unpack(kv_piece)
        key_count = kv_piece.shape[0]
        allowed = key_allowed(key_start, key_count)
        scores = jnp.einsum("hqd,khd->hqk", head_q, keys_here, precision=EXACT) * inv_root
        key_probs = jnp.where(allowed, jnp.exp(scores - log_sums[..., None]), 0.0)
        grad_v = jnp.einsum("hqk,hqd->khd", key_probs, grad_heads, precision=EXACT)
        grad_p = jnp.einsum("hqd,khd->hqk", grad_heads, values_here, precision=EXACT)
        grad_s = key_probs * (grad_p - deltas[..., None]) * inv_root
        grad_q = grad_q + jnp.einsum("hqk,khd->hqd", grad_s, keys_here, precision=EXACT)
        grad_k = jnp.einsum("hqk,hqd->khd", grad_s, head_q, precision=EXACT)
        return (
            grad_q,
            jnp.concatenate(
                [grad_k.reshape(key_count, split_at), grad_v.reshape(key_count, split_at)], axis=1
            ),
        )

    ctx_count = lax.axis_size("ctx")
    ctx_rank = lax.axis_index("ctx")
    grad_zero = jnp.zeros((local_heads, block_len, HD), jnp.float32)

    def cycle_turn(step_index, cycle_state):
        kv_now, grad_kv, grad_q = cycle_state
        owner_rank = (ctx_rank - step_index.astype(jnp.int32)) % ctx_count
        grad_q, grad_part = key_grads(grad_q, kv_now, owner_rank * block_len)
        kv_now, grad_kv = shifted((kv_now, grad_kv + grad_part), "ctx", 1)
        return (kv_now, grad_kv, grad_q)

    kv_now, grad_kv, grad_q = lax.fori_loop(
        0, ctx_count - 1, cycle_turn, (kv_pack, jnp.zeros_like(kv_pack), grad_zero)
    )
    grad_q, grad_part = key_grads(grad_q, kv_now, (ctx_rank + 1) % ctx_count * block_len)
    grad_kv = shifted(grad_kv + grad_part, "ctx", 1)
    grad_keys = grad_kv[:, :split_at].reshape(block_len, local_heads, HD)
    grad_values = grad_kv[:, split_at:].reshape(block_len, local_heads, HD)
    grad_query = jnp.transpose(grad_q, (1, 0, 2))
    grad_proj = jnp.stack([grad_query, grad_keys, grad_values], axis=2).reshape(
        block_len, 3 * split_at
    )
    d_wqkv = jnp.dot(tokens.T, grad_proj, precision=EXACT)
    d_bquery = jnp.sum(grad_query, axis=0).reshape(-1)
    d_bvalue = jnp.sum(grad_values, axis=0).reshape(-1)
    d_inputs = grad_mid + lax.psum(jnp.dot(grad_proj, wide_qkv.T, precision=EXACT), "tp")
    d_wqkv, d_wout, d_wup, d_wdown = (
        lax.psum_scatter(d_wqkv, ("fsdp", "ctx"), scatter_dimension=0, tiled=True),
        lax.psum_scatter(d_wout, ("fsdp", "ctx"), scatter_dimension=1, tiled=True),
        lax.psum_scatter(d_wup, ("fsdp", "ctx"), scatter_dimension=0, tiled=True),
        lax.psum_scatter(d_wdown, ("fsdp", "ctx"), scatter_dimension=1, tiled=True),
    )
    small_sums = lax.psum(
        (d_bquery, d_bvalue, d_bout, d_gattn, d_sattn, d_bup, d_bdown, d_gffn, d_sffn),
        ("fsdp", "ctx"),
    )
    return (
        outputs.reshape(1, block_len, model_width),
        d_inputs.reshape(1, block_len, model_width),
        d_wqkv,
        small_sums[0],
        small_sums[1],
        d_wout,
        small_sums[2],
        small_sums[3],
        small_sums[4],
        d_wup,
        small_sums[5],
        d_wdown,
        small_sums[6],
        small_sums[7],
        small_sums[8],
    )


def solution(mesh):
    in_specs = (
        P("fsdp", "ctx", None),
        P("fsdp"),
        P(("fsdp", "ctx"), "tp"),
        P("tp"),
        P("tp"),
        P("tp", ("fsdp", "ctx")),
        P(),
        P(),
        P(),
        P(("fsdp", "ctx"), "tp"),
        P("tp"),
        P("tp", ("fsdp", "ctx")),
        P(),
        P(),
        P(),
        P("fsdp", "ctx", None),
    )
    out_specs = (
        P("fsdp", "ctx", None),
        P("fsdp", "ctx", None),
        P(("fsdp", "ctx"), "tp"),
        P("tp"),
        P("tp"),
        P("tp", ("fsdp", "ctx")),
        P(),
        P(),
        P(),
        P(("fsdp", "ctx"), "tp"),
        P("tp"),
        P("tp", ("fsdp", "ctx")),
        P(),
        P(),
        P(),
    )
    return jax.shard_map(
        per_device, mesh=mesh, in_specs=in_specs, out_specs=out_specs, check_vma=False
    )
```

profile of v0, /device:TPU:0, one launch (start us, length us, event | category | flops | bytes accessed | tf_op | source)
XLA Modules:
  0.0 1016.2 jit_solution(8169995271465588809)
XLA Ops:
  9.7 51.0 %all-gather.5.cloned.1.call-done = f32[768,576]{1,0:T(8,128)} async-done(((f32[96,576]{1,0:T(8,128)}), f32[768,576]{1,0:T(8,128)}) %all-gather.5.cloned.1.call-update) | async-done | bytes 1769488 | tf_op jit(solution)/shard_map/all_gather | solution.py:54
  60.7 8.3 fusion.40
  71.3 33.2 %all_gather.17 = f32[192,768]{0,1:T(8,128)S(1)} all-gather(f32[192,96]{0,1:T(8,128)S(1)} %copy.39), channel_id=1, replica_groups=mesh['fsdp'=4,'ctx'=2,'tp'=4] {'fsdp','ctx'}, dimensions={1}, use_global_device_ids=true | all-gather | bytes 663552 | tf_op jit(solution)/shard_map/all_gather | solution.py:55
  104.5 20.8 %all-gather.7.cloned.1.call-done = f32[2048,384]{0,1:T(8,128)} async-done(((f32[1024,384]{0,1:T(8,128)}), f32[2048,384]{0,1:T(8,128)}) %all-gather.7.cloned.1.call-update) | async-done | bytes 3145744 | tf_op jit(solution)/shard_map/all_gather | solution.py:83
  127.4 22.5 %fusion = (f32[3,1024]{1,0:T(4,128)S(1)}, f32[3,1024,2048]{2,1,0:T(8,128)S(1)}) fusion(pred[2048]{0:T(1024)(128)(4,1)S(1)} %iota_compare_fusion, f32[2048,3,64]{0,2,1:T(8,128)S(1)} %bitcast.141, f32[1024,3,3,64]{0,3,2,1:T(8,128)S(1)} %bitcast.122), kind=kOutput, calls=%fused_computation.2 | convolution fusion | flops 4850709504 | bytes 27539456 | tf_op jit(solution)/shard_map/hqd,khd->hqk/dot_general | solution.py:87
  150.0 6.5 fusion.1
  158.3 44.2 %bitcast_divide_fusion = (f32[1024,3,64]{0,2,1:T(8,128)S(1)}, f32[3,1024,64]{1,2,0:T(8,128)}) fusion(f32[1024,3]{0,1:T(4,128)S(1)} %bitcast.154, f32[2048,3,64]{0,2,1:T(8,128)S(1)} %bitcast.151, f32[3,1024,2048]{2,1,0:T(8,128)} %copy-done.3, f32[3,1024]{1,0:T(4,128)S(1)} %broadcast_maximum_fusion, pred[2048]{0:T(1024)(128)(4,1)S(1)} %iota_compare_fusion), kind=kOutput, calls=%fused_computation.96 | convolution fusion | flops 4857200640 | bytes 28338176 | tf_op jit(solution)/shard_map/hqk,khd->hqd/dot_general | solution.py:92
  203.4 6.7 fusion.89
  211.4 66.8 %all-reduce.6.cloned.1.call-done = f32[1024,768]{1,0:T(8,128)} async-done(((f32[1024,768]{1,0:T(8,128)}), f32[1024,768]{1,0:T(8,128)}) %all-reduce.6.cloned.1.call-update) | async-done | bytes 3145744 | tf_op jit(solution)/shard_map/psum | solution.py:97
  278.1 3.3 fusion.83
  281.9 50.2 %all-gather.9.cloned.1.call-done = f32[768,768]{1,0:T(8,128)} async-done(((f32[96,768]{1,0:T(8,128)}), f32[768,768]{1,0:T(8,128)}) %all-gather.9.cloned.1.call-update) | async-done | bytes 2359312 | tf_op jit(solution)/shard_map/all_gather | solution.py:56
  332.1 18.5 %fusion.18 = (f32[1024,768]{1,0:T(8,128)}, f32[1024,768]{1,0:T(8,128)}) fusion(f32[768]{0:T(1024)S(1)} %copy-done.31, f32[768,768]{1,0:T(8,128)} %all-gather.9.cloned.1.call-done, f32[1024,768]{1,0:T(8,128)S(1)} %get-tuple-element.115, f32[768]{0:T(1024)S(1)} %copy-done.38, f32[768]{0:T(1024)S(1)} %copy-done.33, f32[1024]{0:T(1024)S(1)} %fusion.69, ...), kind=kOutput, calls=%fused_computation.27 | convolution fusion | flops 7300448256 | bytes 11813888 | tf_op jit(solution)/shard_map/dot_general | solution.py:99
  350.6 33.9 %all-gather.11.cloned.1.call-done = f32[768,768]{0,1:T(8,128)} async-done(((f32[768,96]{0,1:T(8,128)}), f32[768,768]{0,1:T(8,128)}) %all-gather.11.cloned.1.call-update) | async-done | bytes 2359312 | tf_op jit(solution)/shard_map/all_gather | solution.py:57
  384.5 11.9 %fusion.63 = f32[1024,768]{1,0:T(8,128)} fusion(f32[768,768]{0,1:T(8,128)} %all-gather.11.cloned.1.call-done, f32[1024,768]{1,0:T(8,128)} %get-tuple-element.133, f32[1024,768]{1,0:T(8,128)} %get-tuple-element.134, f32[768]{0:T(1024)S(1)} %copy-done.31), kind=kOutput, calls=%fused_computation.93 | convolution fusion | flops 7250116608 | bytes 11799552 | tf_op jit(solution)/shard_map/dot_general | solution.py:102
  397.1 2.7 fusion.87
  399.9 63.7 %all-reduce.8.cloned.1.call-done = f32[1024,768]{1,0:T(8,128)} async-done(((f32[1024,768]{1,0:T(8,128)}), f32[1024,768]{1,0:T(8,128)}) %all-reduce.8.cloned.1.call-update) | async-done | bytes 3145744 | tf_op jit(solution)/shard_map/psum | solution.py:102
  463.6 2.9 fusion.82
  469.5 2.9 fusion.81
  475.3 9.2 fusion.88
  486.2 9.8 fusion.90
  496.1 14.1 %fusion.67 = f32[3,1024,1024]{2,1,0:T(8,128)} fusion(f32[1024,3,64]{0,2,1:T(8,128)} %bitcast.139, f32[1024,3,3,64]{0,3,2,1:T(8,128)} %bitcast.123), kind=kOutput, calls=%fused_computation.101 | convolution fusion | flops 2415919104 | bytes 14155776 | tf_op jit(solution)/shard_map/while/body/eval_jaxpr/hqd,khd->hqk/dot_general | solution.py:125
  510.2 2.5 fusion.86
  512.7 13.6 %fusion.66 = f32[3,1024,1024]{2,1,0:T(8,128)} fusion(f32[1024,3,64]{0,2,1:T(8,128)S(1)} %bitcast.137, f32[1024,3,3,64]{0,3,2,1:T(8,128)} %bitcast.124), kind=kOutput, calls=%fused_computation.100 | convolution fusion | flops 2415919104 | bytes 14155776 | tf_op jit(solution)/shard_map/hqd,khd->hqk/dot_general | solution.py:125
  526.3 38.5 %all-reduce.10.cloned.1.call-done = f32[1024,768]{1,0:T(8,128)} async-done(((f32[1024,768]{1,0:T(8,128)}), f32[1024,768]{1,0:T(8,128)}) %all-reduce.10.cloned.1.call-update) | async-done | bytes 3145744 | tf_op jit(solution)/shard_map/psum | solution.py:111
  564.8 3.9 multiply_reduce_fusion
  570.2 3.7 fusion.32
  574.2 10.5 %fusion.8 = f32[3,64,1024]{2,1,0:T(8,128)} fusion(f32[3,1024,64]{1,2,0:T(8,128)S(1)} %bitcast.130, f32[3,1024,1024]{2,1,0:T(8,128)S(1)} %bitcast.120, f32[3,1024]{1,0:T(4,128)S(1)} %log_add_fusion, pred[1024]{0:T(1024)(128)(4,1)S(1)} %add_compare_fusion.1), kind=kOutput, calls=%fused_computation.14 | convolution fusion | flops 2425356288 | bytes 14169088 | tf_op jit(solution)/shard_map/while/body/eval_jaxpr/hqk,hqd->khd/dot_general | solution.py:127
  584.7 16.0 %multiply_multiply_fusion.1 = f32[3,1024,1024]{2,1,0:T(8,128)S(1)} fusion(f32[3,1024,1024]{2,1,0:T(8,128)} %fusion.67, f32[3,1024]{1,0:T(4,128)S(1)} %multiply_reduce_fusion.5, f32[3,1024]{1,0:T(4,128)S(1)} %log_add_fusion, pred[1024]{0:T(1024)(128)(4,1)S(1)} %add_compare_fusion.1, f32[3,1024,64]{1,2,0:T(8,128)S(1)} %bitcast.131, ...), kind=kOutput, calls=%fused_computation.7 | convolution fusion | flops 2434793472 | bytes 26764288 | tf_op jit(solution)/shard_map/while/body/eval_jaxpr/hqd,khd->hqk/dot_general | solution.py:128
  600.7 9.5 fusion.65
  613.1 13.0 %multiply_multiply_fusion = f32[3,1024,1024]{2,1,0:T(8,128)S(1)} fusion(f32[3,1024,1024]{2,1,0:T(8,128)S(1)} %bitcast.118, f32[3,1024]{1,0:T(4,128)S(1)} %multiply_reduce_fusion.5, f32[3,1024]{1,0:T(4,128)S(1)} %log_add_fusion, pred[1024]{0:T(1024)(128)(4,1)S(1)} %add_compare_fusion, f32[3,1024,64]{1,2,0:T(8,128)S(1)} %bitcast.132, ...), kind=kOutput, calls=%fused_computation.5 | convolution fusion | flops 2434793472 | bytes 26764288 | tf_op jit(solution)/shard_map/hqd,khd->hqk/dot_general | solution.py:128
  626.1 9.6 fusion.64
  635.8 10.5 %fusion.9 = f32[3,64,1024]{2,1,0:T(8,128)} fusion(f32[3,1024,64]{1,2,0:T(8,128)S(1)} %bitcast.133, f32[3,1024,1024]{2,1,0:T(8,128)S(1)} %bitcast.118, f32[3,1024]{1,0:T(4,128)S(1)} %log_add_fusion, pred[1024]{0:T(1024)(128)(4,1)S(1)} %add_compare_fusion), kind=kOutput, calls=%fused_computation.15 | convolution fusion | flops 2425356288 | bytes 14169088 | tf_op jit(solution)/shard_map/hqk,hqd->khd/dot_general | solution.py:127
  647.8 3.2 maximum_add_fusion
  652.5 6.5 fusion.60
  659.1 15.5 %fusion.91 = f32[3,1024,64]{1,2,0:T(8,128)S(1)} fusion(f32[3,1024,1024]{2,1,0:T(8,128)} %copy-done, f32[1024,3,64]{0,2,1:T(8,128)S(1)} %bitcast.140), kind=kOutput, calls=%fused_computation.139 | convolution fusion | flops 2415919104 | bytes 14155776 | tf_op jit(solution)/shard_map/while/body/eval_jaxpr/hqk,khd->hqd/dot_general | solution.py:130
  674.7 12.4 %bitcast_reduce_fusion = (f32[3,64]{1,0:T(4,128)S(1)}, f32[3,1024,64]{1,2,0:T(8,128)S(1)}) fusion(f32[3,1024,64]{1,2,0:T(8,128)S(1)} %fusion.91, f32[3,1024,1024]{2,1,0:T(8,128)S(1)} %copy-done.2, f32[1024,3,64]{0,2,1:T(8,128)S(1)} %bitcast.138), kind=kOutput, calls=%fused_computation.95 | convolution fusion | flops 2416312064 | bytes 14942976 | tf_op jit(solution)/shard_map/hqk,khd->hqd/dot_general | solution.py:130
  691.7 14.8 %fusion.92 = f32[1024,768]{1,0:T(8,128)} fusion(f32[1024,576]{0,1:T(8,128)S(1)} %bitcast.127, f32[768,576]{1,0:T(8,128)S(1)} %copy-done.19), kind=kOutput, calls=%fused_computation.140 | convolution fusion | flops 5435817984 | bytes 7274496 | tf_op jit(solution)/shard_map/dot_general | solution.py:164
  708.4 11.7 %fusion.43 = f32[768,768]{1,0:T(8,128)} fusion(f32[1024,768]{1,0:T(8,128)} %copy-done.24, f32[1024,768]{1,0:T(8,128)S(1)} %copy-done.5, f32[768]{0:T(1024)S(1)} %copy-done.38, f32[768]{0:T(1024)S(1)} %copy-done.33, f32[1024]{0:T(1024)S(1)} %fusion.69, f32[1024]{0:T(1024)S(1)} %broadcast_multiply_fusion.1), kind=kOutput, calls=%fused_computation.74 | convolution fusion | flops 7250903040 | bytes 8665088 | tf_op jit(solution)/shard_map/dot_general | solution.py:109
  720.3 12.9 %fusion.34 = f32[768,768]{0,1:T(8,128)} fusion(f32[1024,768]{1,0:T(8,128)} %copy-done.12, f32[1024]{0:T(1024)S(1)} %negate_multiply_fusion.2, f32[1024,768]{1,0:T(8,128)} %get-tuple-element.133, f32[1024,768]{1,0:T(8,128)} %get-tuple-element.134, f32[768]{0:T(1024)S(1)} %copy-done.31), kind=kOutput, calls=%fused_computation.67 | convolution fusion | flops 7250903040 | bytes 11803648 | tf_op jit(solution)/shard_map/dot_general | solution.py:106
  733.4 8.5 fusion.57
  741.8 2.9 copy.42
  744.7 2.3 reduce_sum.221
  748.7 43.0 %all-reduce.12.cloned.1.call-done = f32[1024,768]{1,0:T(8,128)} async-done(((f32[1024,768]{1,0:T(8,128)}), f32[1024,768]{1,0:T(8,128)}) %all-reduce.12.cloned.1.call-update) | async-done | bytes 3145744 | tf_op jit(solution)/shard_map/psum | solution.py:164
  791.7 4.0 add_reduce_fusion
  795.6 38.1 %all-reduce = (f32[192]{0:T(256)}, f32[192]{0:T(256)}, f32[768]{0:T(1024)}, f32[768]{0:T(1024)}, f32[768]{0:T(1024)}, /*index=5*/f32[768]{0:T(1024)}, f32[768]{0:T(1024)}, f32[768]{0:T(1024)}, f32[768]{0:T(1024)}) all-reduce(f32[192]{0:T(256)S(1)} %reshape.210, ...), channel_id=1, replica_groups=mesh['fsdp'=4,'ctx'=2,'tp'=4] {'fsdp','ctx'}, use_global_device_ids=true, to_apply=%region_17.18 | all-reduce | flops 5760 | bytes 46080 | tf_op jit(solution)/shard_map/psum | solution.py:171
  833.7 31.9 %reduce-scatter.9.cloned.1.call-done = f32[96,768]{1,0:T(8,128)} async-done(((f32[768,768]{1,0:T(8,128)}), f32[96,768]{1,0:T(8,128)}) %reduce-scatter.9.cloned.1.call-update) | async-done | bytes 294928 | tf_op jit(solution)/shard_map/reduce_scatter | solution.py:168
  865.6 72.9 %reduce-scatter.11.cloned.1.call-done = f32[768,96]{0,1:T(8,128)} async-done(((f32[768,768]{0,1:T(8,128)}), f32[768,96]{0,1:T(8,128)}) %reduce-scatter.11.cloned.1.call-update) | async-done | bytes 294928 | tf_op jit(solution)/shard_map/reduce_scatter | solution.py:169
  938.5 70.7 %reduce-scatter.13.cloned.1.call-done = f32[96,576]{1,0:T(8,128)} async-done(((f32[768,576]{1,0:T(8,128)}), f32[96,576]{1,0:T(8,128)}) %reduce-scatter.13.cloned.1.call-update) | async-done | bytes 221200
  (156 shorter events, 35.0 us)
Async XLA Ops:
  7.2 53.5 %all-gather.5.cloned.1.call-start = ((), (), s32[]{:S(2)}) async-start(), calls=%async_computation.4 | async-start | bytes 2211840 | tf_op jit(solution)/shard_map/all_gather | solution.py:54
  7.9 117.4 %all-gather.7.cloned.1.call-start = ((), (), s32[]{:S(2)}) async-start(), calls=%async_computation.5 | async-start | bytes 4718592 | tf_op jit(solution)/shard_map/all_gather | solution.py:83
  69.0 58.4 %copy-start.9 = (f32[1024,576]{0,1:T(8,128)}, f32[1024,576]{0,1:T(8,128)S(1)}, u32[]{:S(2)}) copy-start(f32[1024,576]{0,1:T(8,128)S(1)} %fusion.40) | copy-start | bytes 7077892
  70.5 207.7 %all-reduce.6.cloned.1.call-start = ((), (), s32[]{:S(2)}) async-start(), calls=%async_computation.6 | async-start | bytes 6291456 | tf_op jit(solution)/shard_map/psum | solution.py:97
  104.5 98.0 %copy-start.20 = (f32[192,768]{0,1:T(8,128)}, f32[192,768]{0,1:T(8,128)S(1)}, u32[]{:S(2)}) copy-start(f32[192,768]{0,1:T(8,128)S(1)} %all_gather.17) | copy-start | bytes 1769476
  150.0 8.3 copy-start.3
  203.4 74.7 %copy-start.35 = (f32[768]{0:T(1024)S(1)}, f32[768]{0:T(1024)}, u32[]{:S(2)}) copy-start(f32[768]{0:T(1024)} %param.22) | copy-start | bytes 9220
  210.1 122.0 %all-gather.9.cloned.1.call-start = ((), (), s32[]{:S(2)}) async-start(), calls=%async_computation.7 | async-start | bytes 2654208 | tf_op jit(solution)/shard_map/all_gather | solution.py:56
  210.7 173.8 %all-gather.11.cloned.1.call-start = ((), (), s32[]{:S(2)}) async-start(), calls=%async_computation.8 | async-start | bytes 2654208 | tf_op jit(solution)/shard_map/all_gather | solution.py:57
  211.3 252.2 %all-reduce.8.cloned.1.call-start = ((), (), s32[]{:S(2)}) async-start(), calls=%async_computation.9 | async-start | bytes 6291456 | tf_op jit(solution)/shard_map/psum | solution.py:102
  281.4 287.3 %copy-start.4 = (f32[1024,768]{1,0:T(8,128)}, f32[1024,768]{1,0:T(8,128)S(1)}, u32[]{:S(2)}) copy-start(f32[1024,768]{1,0:T(8,128)S(1)} %get-tuple-element.115) | copy-start | bytes 9437188
  281.4 50.7 %copy-start.31 = (f32[768]{0:T(1024)S(1)}, f32[768]{0:T(1024)}, u32[]{:S(2)}) copy-start(f32[768]{0:T(1024)} %param.26) | copy-start | bytes 9220
  281.4 50.7 %copy-start.33 = (f32[768]{0:T(1024)S(1)}, f32[768]{0:T(1024)}, u32[]{:S(2)}) copy-start(f32[768]{0:T(1024)} %param.23) | copy-start | bytes 9220
  281.4 50.7 %copy-start.38 = (f32[768]{0:T(1024)S(1)}, f32[768]{0:T(1024)}, u32[]{:S(2)}) copy-start(f32[768]{0:T(1024)} %param.24) | copy-start | bytes 9220
  396.4 67.2 %copy-start.36 = (f32[768]{0:T(1024)S(1)}, f32[768]{0:T(1024)}, u32[]{:S(2)}) copy-start(f32[768]{0:T(1024)} %param.28) | copy-start | bytes 9220
  396.4 168.3 %all-reduce.10.cloned.1.call-start = ((), (), s32[]{:S(2)}) async-start(), calls=%async_computation.10 | async-start | bytes 6291456 | tf_op jit(solution)/shard_map/psum | solution.py:111
  396.5 113.7 %collective-permute-start = (f32[1024,384]{0,1:T(8,128)}, f32[1024,384]{0,1:T(8,128)}, u32[]{:S(2)}, u32[]{:S(2)}) collective-permute-start(f32[1024,384]{0,1:T(8,128)} %bitcast.135), channel_id=1, source_target_pairs={{4,0},{0,4},{5,1},{1,5},{6,2},{2,6},{7,3},{3,7},{12,8},{8,12},{13,... | collective-permute-start | bytes 4718600 | tf_op jit(solution)/shard_map/while/body/eval_jaxpr/ppermute | solution.py:15
  469.5 4.1 copy-start.14
  469.5 5.8 copy-start.28
  472.4 12.1 %copy-start.12 = (f32[1024,768]{1,0:T(8,128)}, f32[1024,768]{1,0:T(8,128)S(1)}, u32[]{:S(2)}) copy-start(f32[1024,768]{1,0:T(8,128)S(1)} %get-tuple-element.111) | copy-start | bytes 9437188
  475.3 10.9 %copy-start.27 = (f32[768,768]{1,0:T(8,128)S(1)}, f32[768,768]{1,0:T(8,128)}, u32[]{:S(2)}) copy-start(f32[768,768]{1,0:T(8,128)} %all-gather.9.cloned.1.call-done) | copy-start | bytes 7077892
  496.1 251.0 %reduce-scatter.15.cloned.1.call-start = ((), (), s32[]{:S(2)}) async-start(), calls=%async_computation.15 | async-start | bytes 884736
  512.7 13.6 %copy-start.16 = (f32[1024,192]{0,1:T(8,128)}, f32[1024,192]{0,1:T(8,128)S(1)}, u32[]{:S(2)}) copy-start(f32[1024,192]{0,1:T(8,128)S(1)} %get-tuple-element.126) | copy-start | bytes 2359300
  564.8 9.4 slice-start.3
  564.8 9.4 slice-start.4
  568.7 5.5 slice-start.5
  570.2 3.9 copy-start.6
  570.2 3.7 copy-start.29
  574.2 10.5 %copy-start.22 = (f32[1024,192]{0,1:T(8,128)S(1)}, f32[1024,192]{0,1:T(8,128)}, u32[]{:S(2)}) copy-start(f32[1024,192]{0,1:T(8,128)} %get-tuple-element.127) | copy-start | bytes 2359300
  584.7 28.4 %slice-start = ((s8[12582912]{0:T(1024)(128)(4,1)}), s8[4194304]{0:T(1024)(128)(4,1)S(1)}, s32[]{:S(2)}) async-start(s8[12582912]{0:T(1024)(128)(4,1)} %bitcast.117), calls=%async_computation.16 | async-start | bytes 8388608
  584.7 28.4 %slice-start.1 = ((s8[12582912]{0:T(1024)(128)(4,1)}), s8[4194304]{0:T(1024)(128)(4,1)S(1)}, s32[]{:S(2)}) async-start(s8[12582912]{0:T(1024)(128)(4,1)} %bitcast.117), calls=%async_computation.17 | async-start | bytes 8388608
  584.7 28.4 %slice-start.2 = ((s8[12582912]{0:T(1024)(128)(4,1)}), s8[4194304]{0:T(1024)(128)(4,1)S(1)}, s32[]{:S(2)}) async-start(s8[12582912]{0:T(1024)(128)(4,1)} %bitcast.117), calls=%async_computation.18 | async-start | bytes 8388608
  600.7 9.5 copy-start
  600.7 9.5 copy-start.30
  611.6 36.2 %collective-permute-start.1 = (f32[1024,384]{0,1:T(8,128)}, f32[1024,384]{0,1:T(8,128)}, u32[]{:S(2)}, u32[]{:S(2)}) collective-permute-start(f32[1024,384]{0,1:T(8,128)} %pad_maximum_fusion.1), channel_id=1, source_target_pairs={{4,0},{0,4},{5,1},{1,5},{6,2},{2,6},{7,3},{3,7},{12,8},{8,12},{13,... | collective-permute-start | bytes 4718600 | tf_op jit(solution)/shard_map/while/body/eval_jaxpr/ppermute | solution.py:15
  626.1 9.6 copy-start.1
  646.3 6.2 copy-start.7
  646.3 6.2 copy-start.26
  651.0 8.1 copy-start.18
  651.0 38.1 %collective-permute-start.2 = (f32[1024,384]{0,1:T(8,128)}, f32[1024,384]{0,1:T(8,128)S(1)}, u32[]{:S(2)}, u32[]{:S(2)}) collective-permute-start(f32[1024,384]{0,1:T(8,128)} %maximum_add_fusion), channel_id=1, source_target_pairs={{4,0},{0,4},{5,1},{1,5},{6,2},{2,6},{7,3},{3,7},{12,8},{8,12},{13,... | collective-permute-start | bytes 4718600 | tf_op jit(solution)/shard_map/ppermute | solution.py:15
  659.0 15.6 %copy-start.17 = (f32[1024,192]{0,1:T(8,128)S(1)}, f32[1024,192]{0,1:T(8,128)}, u32[]{:S(2)}) copy-start(f32[1024,192]{0,1:T(8,128)} %copy-done.16) | copy-start | bytes 2359300
  659.1 132.6 %all-reduce.12.cloned.1.call-start = ((), (), s32[]{:S(2)}) async-start(), calls=%async_computation.11 | async-start | bytes 6291456 | tf_op jit(solution)/shard_map/psum | solution.py:164
  659.1 15.5 %copy-start.2 = (f32[3,1024,1024]{2,1,0:T(8,128)S(1)}, f32[3,1024,1024]{2,1,0:T(8,128)}, u32[]{:S(2)}) copy-start(f32[3,1024,1024]{2,1,0:T(8,128)} %copy-done.1) | copy-start | bytes 37748740
  706.5 159.1 %reduce-scatter.9.cloned.1.call-start = ((), (), s32[]{:S(2)}) async-start(), calls=%async_computation.12 | async-start | bytes 2654208 | tf_op jit(solution)/shard_map/reduce_scatter | solution.py:168
  720.1 218.4 %reduce-scatter.11.cloned.1.call-start = ((), (), s32[]{:S(2)}) async-start(), calls=%async_computation.13 | async-start | bytes 2654208 | tf_op jit(solution)/shard_map/reduce_scatter | solution.py:169
  720.3 13.0 %copy-start.10 = (f32[1,1024,768]{2,1,0:T(8,128)S(1)}, f32[1,1024,768]{2,1,0:T(8,128)}, u32[]{:S(2)}) copy-start(f32[1,1024,768]{2,1,0:T(8,128)} %param.16) | copy-start | bytes 9437188
  733.3 275.9 %reduce-scatter.13.cloned.1.call-start = ((), (), s32[]{:S(2)}) async-start(), calls=%async_computation.14 | async-start | bytes 2211840
  744.7 47.0 %copy-start.8 = (f32[1024,768]{1,0:T(8,128)S(1)}, f32[1024,768]{1,0:T(8,128)}, u32[]{:S(2)}) copy-start(f32[1024,768]{1,0:T(8,128)} %copy-done.6) | copy-start | bytes 9437188
  (12 other events, 22.5 us)
Sparse Core Ops, SparseCore 0:
  10.2 50.4 all-gather.4
  70.6 54.7 all-gather.6
  210.3 67.7 all-reduce.5
  280.2 51.9 all-gather.8
  334.1 50.3 all-gather.10
  396.5 66.9 all-reduce.7
  496.2 68.5 all-reduce.9
  659.2 62.5 reduce-scatter.14
  724.1 67.4 all-reduce.11
  795.6 69.9 reduce-scatter.8
  869.7 68.7 reduce-scatter.10
  942.4 66.7 reduce-scatter.12
where the time goes:
time: 1020 us
  waiting for transfers between devices  549 us (54%)
  matrix products  314 us (31%)
  blocking collectives  71.3 us (7%)
  other arithmetic  34.5 us (3%)
  local copies, waits for them, and re-layouts  27.4 us (3%)
  between operations  15.7 us (2%)
    reduce_scatter x1, waiting for transfers between devices, per_device(): lax.psum_scatter(d_wdown, ('fsdp', 'ctx'), scatter_dimension=1, tiled=True)  72.9 us
    unnamed x14, waiting for transfers between devices  72.6 us
    psum x1, waiting for transfers between devices, per_device(): lax.psum(jnp.dot(attended, wide_out, precision=EXACT), 'tp')  66.8 us
    psum x1, waiting for transfers between devices, per_device(): lax.psum(jnp.dot(activated, wide_down, precision=EXACT), 'tp')  63.7 us
    all_gather x1, waiting for transfers between devices, per_device(): lax.all_gather(w_qkv, ('fsdp', 'ctx'), axis=0, tiled=True)  51 us
    all_gather x1, waiting for transfers between devices, per_device(): lax.all_gather(w_up, ('fsdp', 'ctx'), axis=0, tiled=True)  50.2 us
    dot_general x1, matrix products, per_device(): jnp.einsum('hqk,khd->hqd', key_probs, values_here, precision=EXACT)  44.2 us
    psum x1, waiting for transfers between devices, per_device(): lax.psum(jnp.dot(grad_proj, wide_qkv.T, precision=EXACT), 'tp')  43 us
  transfers between devices with their start and end apart: 15, of which 13 were waited for; matrix products, arithmetic and copies ran while one was open for 21% of the time, Pallas kernels for 0%

commit v1 on v0

--- a/solution.py
+++ b/solution.py
@@ -7,6 +7,27 @@
 NORM_EPS = 1e-12
 MASKED = -1e30
 EXACT = lax.Precision.HIGHEST
+
+
+def ring_gather(shard, axis, dim):
+    length, place, extent = (lax.axis_size(axis), lax.axis_index(axis), shard.shape[dim])
+    upward = [(i, (i + 1) % length) for i in range(length)]
+    downward = [(i, (i - 1) % length) for i in range(length)]
+    out = jnp.zeros((*shard.shape[:dim], length * extent, *shard.shape[dim + 1 :]), shard.dtype)
+    out = lax.dynamic_update_slice_in_dim(out, shard, place * extent, axis=dim)
+    from_left = from_right = shard
+    half = length // 2
+    for step in range(1, half + 1):
+        from_left = lax.ppermute(from_left, axis, upward)
+        out = lax.dynamic_update_slice_in_dim(
+            out, from_left, (place - step) % length * extent, axis=dim
+        )
+        if step < length - half:
+            from_right = lax.ppermute(from_right, axis, downward)
+            out = lax.dynamic_update_slice_in_dim(
+                out, from_right, (place + step) % length * extent, axis=dim
+            )
+    return out
 
 
 def shifted(block, axis, distance):
@@ -54,7 +75,7 @@
         lax.all_gather(w_qkv, ("fsdp", "ctx"), axis=0, tiled=True),
         lax.all_gather(w_out, ("fsdp", "ctx"), axis=1, tiled=True),
         lax.all_gather(w_up, ("fsdp", "ctx"), axis=0, tiled=True),
-        lax.all_gather(w_down, ("fsdp", "ctx"), axis=1, tiled=True),
+        ring_gather(w_down, ("fsdp", "ctx"), 1),
     )
     bias_qkv = jnp.stack(
         [

time: 1020 us -> 974 us (0.955)
  waiting for transfers between devices: 549 us -> 494 us
  starting transfers between devices: 4.63 us -> 21.5 us
  matrix products: 314 us -> 298 us
    psum x1, waiting for transfers between devices: 66.8 us -> 14 us  [per_device(): lax.psum(jnp.dot(attended, wide_out, precision=EXACT), 'tp')]
    all_gather x1 -> x0, waiting for transfers between devices: 33.9 us -> none  [per_device(): lax.all_gather(w_down, ('fsdp', 'ctx'), axis=1, tiled=True)]
    ppermute x0 -> x7, waiting for transfers between devices: none -> 32.5 us  [the longest x4 32.5 us: ring_gather(): from_left = lax.ppermute(from_left, axis, upward)]
    ppermute x0 -> x7, starting transfers between devices: none -> 16.9 us  [the longest x3 8.51 us: ring_gather(): from_right = lax.ppermute(from_right, axis, downward)]
    dot_general x1, matrix products: 44.2 us -> 32.5 us  [per_device(): jnp.einsum('hqk,khd->hqd', key_probs, values_here, precision=EXACT)]
    unnamed x94 -> x104, local copies, waits for them, and re-layouts: 17.9 us -> 21.8 us
    unnamed x14 -> x13, waiting for transfers between devices: 72.6 us -> 72.2 us
  transfers between devices with their start and end apart: 15 -> 21, of which waited for: 13 -> 16; matrix products, arithmetic and copies ran while one was open for 21% -> 20% of each run, Pallas kernels for 0% -> 0%
where the time goes in v1:
time: 974 us; the launch traced here: 968 us
  waiting for transfers between devices  494 us (51%)
  matrix products  298 us (31%)
  blocking collectives  71.1 us (7%)
  other arithmetic  34.4 us (4%)
  local copies, waits for them, and re-layouts  33.6 us (3%)
  starting transfers between devices  21.5 us (2%)
  between operations  15.6 us (2%)
    reduce_scatter x1, waiting for transfers between devices, per_device(): lax.psum_scatter(d_wdown, ('fsdp', 'ctx'), scatter_dimension=1, tiled=True)  72.7 us
    unnamed x13, waiting for transfers between devices  72.2 us
    psum x1, waiting for transfers between devices, per_device(): lax.psum(jnp.dot(activated, wide_down, precision=EXACT), 'tp')  63.7 us
    all_gather x1, waiting for transfers between devices, per_device(): lax.all_gather(w_qkv, ('fsdp', 'ctx'), axis=0, tiled=True)  51 us
    all_gather x1, waiting for transfers between devices, per_device(): lax.all_gather(w_up, ('fsdp', 'ctx'), axis=0, tiled=True)  50.2 us
    psum x1, waiting for transfers between devices, per_device(): lax.psum(jnp.dot(grad_proj, wide_qkv.T, precision=EXACT), 'tp')  42.9 us
    psum x1, waiting for transfers between devices, per_device(): lax.psum(jnp.dot(grad_pre, wide_up.T, precision=EXACT), 'tp')  38.5 us
    psum x1, blocking collectives, per_device(): lax.psum((d_bquery, d_bvalue, d_bout, d_gattn, d_sattn, d_bup, d_bdown, d...  37.9 us
  transfers between devices with their start and end apart: 21, of which 16 were waited for; matrix products, arithmetic and copies ran while one was open for 20% of the time, Pallas kernels for 0%

profile of v1, /device:TPU:0, one launch (start us, length us, event | category | flops | bytes accessed | tf_op | source)
XLA Modules:
  0.0 968.2 jit_solution(12497317092116012581)
XLA Ops:
  9.7 51.0 %all-gather.4.cloned.1.call-done = f32[768,576]{1,0:T(8,128)} async-done(((f32[96,576]{1,0:T(8,128)}), f32[768,576]{1,0:T(8,128)}) %all-gather.4.cloned.1.call-update) | async-done | bytes 1769488 | tf_op jit(solution)/shard_map/all_gather | solution.py:75
  60.7 8.3 fusion.40
  71.3 33.2 %all_gather.14 = f32[192,768]{0,1:T(8,128)S(1)} all-gather(f32[192,96]{0,1:T(8,128)S(1)} %copy.39), channel_id=1, replica_groups=mesh['fsdp'=4,'ctx'=2,'tp'=4] {'fsdp','ctx'}, dimensions={1}, use_global_device_ids=true | all-gather | bytes 663552 | tf_op jit(solution)/shard_map/all_gather | solution.py:76
  104.5 20.8 %all-gather.6.cloned.1.call-done = f32[2048,384]{0,1:T(8,128)} async-done(((f32[1024,384]{0,1:T(8,128)}), f32[2048,384]{0,1:T(8,128)}) %all-gather.6.cloned.1.call-update) | async-done | bytes 3145744 | tf_op jit(solution)/shard_map/all_gather | solution.py:104
  127.4 22.3 %fusion = (f32[3,1024]{1,0:T(4,128)S(1)}, f32[3,1024,2048]{2,1,0:T(8,128)S(1)}) fusion(pred[2048]{0:T(1024)(128)(4,1)S(1)} %iota_compare_fusion, f32[2048,3,64]{0,2,1:T(8,128)S(1)} %bitcast.141, f32[1024,3,3,64]{0,3,2,1:T(8,128)S(1)} %bitcast.122), kind=kOutput, calls=%fused_computation.2 | convolution fusion | flops 4850709504 | bytes 27539456 | tf_op jit(solution)/shard_map/hqd,khd->hqk/dot_general | solution.py:108
  149.8 6.5 fusion.1
  158.0 32.5 %bitcast_divide_fusion = (f32[1024,3,64]{0,2,1:T(8,128)S(1)}, f32[3,1024,64]{1,2,0:T(8,128)}) fusion(f32[1024,3]{0,1:T(4,128)S(1)} %bitcast.154, f32[2048,3,64]{0,2,1:T(8,128)S(1)} %bitcast.151, f32[3,1024,2048]{2,1,0:T(8,128)} %copy-done.3, f32[3,1024]{1,0:T(4,128)S(1)} %broadcast_maximum_fusion, pred[2048]{0:T(1024)(128)(4,1)S(1)} %iota_compare_fusion), kind=kOutput, calls=%fused_computation.96 | convolution fusion | flops 4857200640 | bytes 28338176 | tf_op jit(solution)/shard_map/hqk,khd->hqd/dot_general | solution.py:113
  191.4 6.7 fusion.89
  199.6 4.0 collective-permute-start.1
  203.6 8.6 collective-permute-done
  217.3 9.6 collective-permute-done.2
  232.7 8.2 collective-permute-done.4
  244.6 6.1 collective-permute-done.6
  252.1 14.0 %all-reduce.6.cloned.1.call-done = f32[1024,768]{1,0:T(8,128)} async-done(((f32[1024,768]{1,0:T(8,128)}), f32[1024,768]{1,0:T(8,128)}) %all-reduce.6.cloned.1.call-update) | async-done | bytes 3145744 | tf_op jit(solution)/shard_map/psum | solution.py:118
  266.2 3.3 fusion.83
  270.0 50.2 %all-gather.8.cloned.1.call-done = f32[768,768]{1,0:T(8,128)} async-done(((f32[96,768]{1,0:T(8,128)}), f32[768,768]{1,0:T(8,128)}) %all-gather.8.cloned.1.call-update) | async-done | bytes 2359312 | tf_op jit(solution)/shard_map/all_gather | solution.py:77
  320.2 16.6 %fusion.18 = (f32[1024,768]{1,0:T(8,128)S(1)}, f32[1024,768]{1,0:T(8,128)S(1)}) fusion(f32[768]{0:T(1024)S(1)} %copy-done.36, f32[768,768]{1,0:T(8,128)} %all-gather.8.cloned.1.call-done, f32[1024,768]{1,0:T(8,128)S(1)} %get-tuple-element.115, f32[768]{0:T(1024)S(1)} %copy-done.43, f32[768]{0:T(1024)S(1)} %copy-done.38, f32[1024]{0:T(1024)S(1)} %fusion.69, ...), kind=kOutput, calls=%fused_computation.27 | convolution fusion | flops 7300448256 | bytes 11813888 | tf_op jit(solution)/shard_map/dot_general | solution.py:120
  339.5 9.5 fusion.63
  352.5 63.7 %all-reduce.8.cloned.1.call-done = f32[1024,768]{1,0:T(8,128)} async-done(((f32[1024,768]{1,0:T(8,128)}), f32[1024,768]{1,0:T(8,128)}) %all-reduce.8.cloned.1.call-update) | async-done | bytes 3145744 | tf_op jit(solution)/shard_map/psum | solution.py:123
  416.2 2.9 fusion.82
  422.1 2.9 fusion.81
  427.9 9.2 fusion.88
  438.7 9.8 %fusion.90 = f32[1024,768]{1,0:T(8,128)} fusion(f32[1024,768]{1,0:T(8,128)S(1)} %get-tuple-element.138, f32[768,768]{1,0:T(8,128)S(1)} %copy-done.32), kind=kOutput, calls=%fused_computation.146 | convolution fusion | flops 7247757312 | bytes 8650752 | tf_op jit(solution)/shard_map/dot_general | solution.py:132
  448.5 14.1 %fusion.67 = f32[3,1024,1024]{2,1,0:T(8,128)} fusion(f32[1024,3,64]{0,2,1:T(8,128)} %bitcast.139, f32[1024,3,3,64]{0,3,2,1:T(8,128)} %bitcast.123), kind=kOutput, calls=%fused_computation.101 | convolution fusion | flops 2415919104 | bytes 14155776 | tf_op jit(solution)/shard_map/while/body/eval_jaxpr/hqd,khd->hqk/dot_general | solution.py:146
  465.1 13.6 %fusion.66 = f32[3,1024,1024]{2,1,0:T(8,128)} fusion(f32[1024,3,64]{0,2,1:T(8,128)S(1)} %bitcast.137, f32[1024,3,3,64]{0,3,2,1:T(8,128)} %bitcast.124), kind=kOutput, calls=%fused_computation.100 | convolution fusion | flops 2415919104 | bytes 14155776 | tf_op jit(solution)/shard_map/hqd,khd->hqk/dot_general | solution.py:146
  478.7 38.5 %all-reduce.10.cloned.1.call-done = f32[1024,768]{1,0:T(8,128)} async-done(((f32[1024,768]{1,0:T(8,128)}), f32[1024,768]{1,0:T(8,128)}) %all-reduce.10.cloned.1.call-update) | async-done | bytes 3145744 | tf_op jit(solution)/shard_map/psum | solution.py:132
  517.2 3.9 multiply_reduce_fusion
  522.7 3.7 fusion.32
  526.6 10.5 %fusion.8 = f32[3,64,1024]{2,1,0:T(8,128)} fusion(f32[3,1024,64]{1,2,0:T(8,128)S(1)} %bitcast.130, f32[3,1024,1024]{2,1,0:T(8,128)S(1)} %bitcast.120, f32[3,1024]{1,0:T(4,128)S(1)} %log_add_fusion, pred[1024]{0:T(1024)(128)(4,1)S(1)} %add_compare_fusion.1), kind=kOutput, calls=%fused_computation.14 | convolution fusion | flops 2425356288 | bytes 14169088 | tf_op jit(solution)/shard_map/while/body/eval_jaxpr/hqk,hqd->khd/dot_general | solution.py:148
  537.1 16.0 %multiply_multiply_fusion.1 = f32[3,1024,1024]{2,1,0:T(8,128)S(1)} fusion(f32[3,1024,1024]{2,1,0:T(8,128)} %fusion.67, f32[3,1024]{1,0:T(4,128)S(1)} %multiply_reduce_fusion.5, f32[3,1024]{1,0:T(4,128)S(1)} %log_add_fusion, pred[1024]{0:T(1024)(128)(4,1)S(1)} %add_compare_fusion.1, f32[3,1024,64]{1,2,0:T(8,128)S(1)} %bitcast.131, ...), kind=kOutput, calls=%fused_computation.7 | convolution fusion | flops 2434793472 | bytes 26764288 | tf_op jit(solution)/shard_map/while/body/eval_jaxpr/hqd,khd->hqk/dot_general | solution.py:149
  553.1 9.5 fusion.65
  565.5 13.0 %multiply_multiply_fusion = f32[3,1024,1024]{2,1,0:T(8,128)S(1)} fusion(f32[3,1024,1024]{2,1,0:T(8,128)S(1)} %bitcast.118, f32[3,1024]{1,0:T(4,128)S(1)} %multiply_reduce_fusion.5, f32[3,1024]{1,0:T(4,128)S(1)} %log_add_fusion, pred[1024]{0:T(1024)(128)(4,1)S(1)} %add_compare_fusion, f32[3,1024,64]{1,2,0:T(8,128)S(1)} %bitcast.132, ...), kind=kOutput, calls=%fused_computation.5 | convolution fusion | flops 2434793472 | bytes 26764288 | tf_op jit(solution)/shard_map/hqd,khd->hqk/dot_general | solution.py:149
  578.5 9.6 fusion.64
  588.1 10.5 %fusion.9 = f32[3,64,1024]{2,1,0:T(8,128)} fusion(f32[3,1024,64]{1,2,0:T(8,128)S(1)} %bitcast.133, f32[3,1024,1024]{2,1,0:T(8,128)S(1)} %bitcast.118, f32[3,1024]{1,0:T(4,128)S(1)} %log_add_fusion, pred[1024]{0:T(1024)(128)(4,1)S(1)} %add_compare_fusion), kind=kOutput, calls=%fused_computation.15 | convolution fusion | flops 2425356288 | bytes 14169088 | tf_op jit(solution)/shard_map/hqk,hqd->khd/dot_general | solution.py:148
  600.2 3.1 maximum_add_fusion
  604.8 6.5 fusion.60
  611.4 15.5 %fusion.91 = f32[3,1024,64]{1,2,0:T(8,128)S(1)} fusion(f32[3,1024,1024]{2,1,0:T(8,128)} %copy-done, f32[1024,3,64]{0,2,1:T(8,128)S(1)} %bitcast.140), kind=kOutput, calls=%fused_computation.147 | convolution fusion | flops 2415919104 | bytes 14155776 | tf_op jit(solution)/shard_map/while/body/eval_jaxpr/hqk,khd->hqd/dot_general | solution.py:151
  627.0 12.4 %bitcast_reduce_fusion = (f32[3,64]{1,0:T(4,128)S(1)}, f32[3,1024,64]{1,2,0:T(8,128)S(1)}) fusion(f32[3,1024,64]{1,2,0:T(8,128)S(1)} %fusion.91, f32[3,1024,1024]{2,1,0:T(8,128)S(1)} %copy-done.2, f32[1024,3,64]{0,2,1:T(8,128)S(1)} %bitcast.138), kind=kOutput, calls=%fused_computation.95 | convolution fusion | flops 2416312064 | bytes 14942976 | tf_op jit(solution)/shard_map/hqk,khd->hqd/dot_general | solution.py:151
  644.0 14.8 %fusion.92 = f32[1024,768]{1,0:T(8,128)} fusion(f32[1024,576]{0,1:T(8,128)S(1)} %bitcast.127, f32[768,576]{1,0:T(8,128)S(1)} %copy-done.24), kind=kOutput, calls=%fused_computation.148 | convolution fusion | flops 5435817984 | bytes 7274496 | tf_op jit(solution)/shard_map/dot_general | solution.py:185
  660.7 11.6 %fusion.43 = f32[768,768]{1,0:T(8,128)} fusion(f32[1024,768]{1,0:T(8,128)} %copy-done.29, f32[1024,768]{1,0:T(8,128)S(1)} %copy-done.5, f32[768]{0:T(1024)S(1)} %copy-done.43, f32[768]{0:T(1024)S(1)} %copy-done.38, f32[1024]{0:T(1024)S(1)} %fusion.69, f32[1024]{0:T(1024)S(1)} %broadcast_multiply_fusion.1), kind=kOutput, calls=%fused_computation.74 | convolution fusion | flops 7250903040 | bytes 8665088 | tf_op jit(solution)/shard_map/dot_general | solution.py:130
  672.5 13.0 %fusion.34 = f32[768,768]{0,1:T(8,128)} fusion(f32[1024,768]{1,0:T(8,128)} %copy-done.12, f32[1024]{0:T(1024)S(1)} %negate_multiply_fusion.2, f32[1024,768]{1,0:T(8,128)} %copy-done.13, f32[1024,768]{1,0:T(8,128)} %copy-done.15, f32[768]{0:T(1024)S(1)} %copy-done.36), kind=kOutput, calls=%fused_computation.67 | convolution fusion | flops 7250903040 | bytes 11803648 | tf_op jit(solution)/shard_map/dot_general | solution.py:127
  685.6 8.5 fusion.57
  701.0 42.9 %all-reduce.12.cloned.1.call-done = f32[1024,768]{1,0:T(8,128)} async-done(((f32[1024,768]{1,0:T(8,128)}), f32[1024,768]{1,0:T(8,128)}) %all-reduce.12.cloned.1.call-update) | async-done | bytes 3145744 | tf_op jit(solution)/shard_map/psum | solution.py:185
  743.9 4.0 add_reduce_fusion
  747.8 37.9 %all-reduce = (f32[192]{0:T(256)}, f32[192]{0:T(256)}, f32[768]{0:T(1024)}, f32[768]{0:T(1024)}, f32[768]{0:T(1024)}, /*index=5*/f32[768]{0:T(1024)}, f32[768]{0:T(1024)}, f32[768]{0:T(1024)}, f32[768]{0:T(1024)}) all-reduce(f32[192]{0:T(256)S(1)} %reshape.210, ...), channel_id=1, replica_groups=mesh['fsdp'=4,'ctx'=2,'tp'=4] {'fsdp','ctx'}, use_global_device_ids=true, to_apply=%region_17.18 | all-reduce | flops 5760 | bytes 46080 | tf_op jit(solution)/shard_map/psum | solution.py:192
  785.7 32.2 %reduce-scatter.9.cloned.1.call-done = f32[96,768]{1,0:T(8,128)} async-done(((f32[768,768]{1,0:T(8,128)}), f32[96,768]{1,0:T(8,128)}) %reduce-scatter.9.cloned.1.call-update) | async-done | bytes 294928 | tf_op jit(solution)/shard_map/reduce_scatter | solution.py:189
  817.9 72.7 %reduce-scatter.11.cloned.1.call-done = f32[768,96]{0,1:T(8,128)} async-done(((f32[768,768]{0,1:T(8,128)}), f32[768,96]{0,1:T(8,128)}) %reduce-scatter.11.cloned.1.call-update) | async-done | bytes 294928 | tf_op jit(solution)/shard_map/reduce_scatter | solution.py:190
  890.6 70.9 %reduce-scatter.13.cloned.1.call-done = f32[96,576]{1,0:T(8,128)} async-done(((f32[768,576]{1,0:T(8,128)}), f32[96,576]{1,0:T(8,128)}) %reduce-scatter.13.cloned.1.call-update) | async-done | bytes 221200
  (186 shorter events, 64.0 us)
Async XLA Ops:
  7.2 53.5 %all-gather.4.cloned.1.call-start = ((), (), s32[]{:S(2)}) async-start(), calls=%async_computation.4 | async-start | bytes 2211840 | tf_op jit(solution)/shard_map/all_gather | solution.py:75
  7.9 117.4 %all-gather.6.cloned.1.call-start = ((), (), s32[]{:S(2)}) async-start(), calls=%async_computation.5 | async-start | bytes 4718592 | tf_op jit(solution)/shard_map/all_gather | solution.py:104
  69.0 58.4 %copy-start.9 = (f32[1024,576]{0,1:T(8,128)}, f32[1024,576]{0,1:T(8,128)S(1)}, u32[]{:S(2)}) copy-start(f32[1024,576]{0,1:T(8,128)S(1)} %fusion.40) | copy-start | bytes 7077892
  70.5 195.7 %all-reduce.6.cloned.1.call-start = ((), (), s32[]{:S(2)}) async-start(), calls=%async_computation.6 | async-start | bytes 6291456 | tf_op jit(solution)/shard_map/psum | solution.py:118
  104.5 86.1 %copy-start.25 = (f32[192,768]{0,1:T(8,128)}, f32[192,768]{0,1:T(8,128)S(1)}, u32[]{:S(2)}) copy-start(f32[192,768]{0,1:T(8,128)S(1)} %all_gather.14) | copy-start | bytes 1769476
  149.7 8.3 copy-start.3
  198.2 122.0 %all-gather.8.cloned.1.call-start = ((), (), s32[]{:S(2)}) async-start(), calls=%async_computation.7 | async-start | bytes 2654208 | tf_op jit(solution)/shard_map/all_gather | solution.py:77
  198.8 217.4 %all-reduce.8.cloned.1.call-start = ((), (), s32[]{:S(2)}) async-start(), calls=%async_computation.8 | async-start | bytes 6291456 | tf_op jit(solution)/shard_map/psum | solution.py:123
  198.8 13.4 %collective-permute-start = (f32[768,96]{0,1:T(8,128)S(1)}, f32[768,96]{0,1:T(8,128)}, u32[]{:S(2)}, u32[]{:S(2)}) collective-permute-start(f32[768,96]{0,1:T(8,128)S(1)} %copy-done.35), channel_id=1, source_target_pairs={{0,4},{4,8},{8,12},{12,16},{16,20},{20,24},{24,28},{28,0},{1,5},{5... | collective-permute-start | bytes 884744 | tf_op jit(solution)/shard_map/ppermute | solution.py:21
  199.6 15.2 %collective-permute-start.1 = (f32[768,96]{0,1:T(8,128)S(1)}, f32[768,96]{0,1:T(8,128)S(1)}, u32[]{:S(2)}, u32[]{:S(2)}) collective-permute-start(f32[768,96]{0,1:T(8,128)S(1)} %copy-done.35), channel_id=1, source_target_pairs={{0,28},{4,0},{8,4},{12,8},{16,12},{20,16},{24,20},{28,24},{1,29},{... | collective-permute-start | bytes 884744 | tf_op jit(solution)/shard_map/ppermute | solution.py:26
  212.2 14.7 %collective-permute-start.2 = (f32[768,96]{0,1:T(8,128)}, f32[768,96]{0,1:T(8,128)S(1)}, u32[]{:S(2)}, u32[]{:S(2)}) collective-permute-start(f32[768,96]{0,1:T(8,128)} %collective-permute-done), channel_id=1, source_target_pairs={{0,4},{4,8},{8,12},{12,16},{16,20},{20,24},{24,28},{28,0},{1,5},{5... | collective-permute-start | bytes 884744 | tf_op jit(solution)/shard_map/ppermute | solution.py:21
  214.8 51.3 %copy-start.40 = (f32[768]{0:T(1024)S(1)}, f32[768]{0:T(1024)}, u32[]{:S(2)}) copy-start(f32[768]{0:T(1024)} %param.22) | copy-start | bytes 9220
  214.8 15.5 %collective-permute-start.3 = (f32[768,96]{0,1:T(8,128)S(1)}, f32[768,96]{0,1:T(8,128)}, u32[]{:S(2)}, u32[]{:S(2)}) collective-permute-start(f32[768,96]{0,1:T(8,128)S(1)} %collective-permute-done.1), channel_id=1, source_target_pairs={{0,28},{4,0},{8,4},{12,8},{16,12},{20,16},{24,20},{28,24},{1,29},{... | collective-permute-start | bytes 884744 | tf_op jit(solution)/shard_map/ppermute | solution.py:26
  226.9 14.0 %collective-permute-start.4 = (f32[768,96]{0,1:T(8,128)S(1)}, f32[768,96]{0,1:T(8,128)S(1)}, u32[]{:S(2)}, u32[]{:S(2)}) collective-permute-start(f32[768,96]{0,1:T(8,128)S(1)} %collective-permute-done.2), channel_id=1, source_target_pairs={{0,4},{4,8},{8,12},{12,16},{16,20},{20,24},{24,28},{28,0},{1,5},{5... | collective-permute-start | bytes 884744 | tf_op jit(solution)/shard_map/ppermute | solution.py:21
  230.3 14.3 %collective-permute-start.5 = (f32[768,96]{0,1:T(8,128)}, f32[768,96]{0,1:T(8,128)S(1)}, u32[]{:S(2)}, u32[]{:S(2)}) collective-permute-start(f32[768,96]{0,1:T(8,128)} %collective-permute-done.3), channel_id=1, source_target_pairs={{0,28},{4,0},{8,4},{12,8},{16,12},{20,16},{24,20},{28,24},{1,29},{... | collective-permute-start | bytes 884744 | tf_op jit(solution)/shard_map/ppermute | solution.py:26
  240.9 9.8 %collective-permute-start.6 = (f32[768,96]{0,1:T(8,128)S(1)}, f32[768,96]{0,1:T(8,128)S(1)}, u32[]{:S(2)}, u32[]{:S(2)}) collective-permute-start(f32[768,96]{0,1:T(8,128)S(1)} %collective-permute-done.4), channel_id=1, source_target_pairs={{0,4},{4,8},{8,12},{12,16},{16,20},{20,24},{24,28},{28,0},{1,5},{5... | collective-permute-start | bytes 884744 | tf_op jit(solution)/shard_map/ppermute | solution.py:21
  269.4 251.6 %copy-start.4 = (f32[1024,768]{1,0:T(8,128)}, f32[1024,768]{1,0:T(8,128)S(1)}, u32[]{:S(2)}) copy-start(f32[1024,768]{1,0:T(8,128)S(1)} %get-tuple-element.115) | copy-start | bytes 9437188
  269.4 50.7 %copy-start.36 = (f32[768]{0:T(1024)S(1)}, f32[768]{0:T(1024)}, u32[]{:S(2)}) copy-start(f32[768]{0:T(1024)} %param.26) | copy-start | bytes 9220
  269.4 50.7 %copy-start.38 = (f32[768]{0:T(1024)S(1)}, f32[768]{0:T(1024)}, u32[]{:S(2)}) copy-start(f32[768]{0:T(1024)} %param.23) | copy-start | bytes 9220
  269.5 50.7 %copy-start.43 = (f32[768]{0:T(1024)S(1)}, f32[768]{0:T(1024)}, u32[]{:S(2)}) copy-start(f32[768]{0:T(1024)} %param.24) | copy-start | bytes 9220
  320.1 19.4 %copy-start.19 = (f32[768,768]{0,1:T(8,128)S(1)}, f32[768,768]{0,1:T(8,128)}, u32[]{:S(2)}) copy-start(f32[768,768]{0,1:T(8,128)} %copy-done.18) | copy-start | bytes 7077892
  349.0 67.2 %copy-start.41 = (f32[768]{0:T(1024)S(1)}, f32[768]{0:T(1024)}, u32[]{:S(2)}) copy-start(f32[768]{0:T(1024)} %param.28) | copy-start | bytes 9220
  349.0 168.2 %all-reduce.10.cloned.1.call-start = ((), (), s32[]{:S(2)}) async-start(), calls=%async_computation.9 | async-start | bytes 6291456 | tf_op jit(solution)/shard_map/psum | solution.py:132
  349.1 113.5 %collective-permute-start.7 = (f32[1024,384]{0,1:T(8,128)}, f32[1024,384]{0,1:T(8,128)}, u32[]{:S(2)}, u32[]{:S(2)}) collective-permute-start(f32[1024,384]{0,1:T(8,128)} %bitcast.135), channel_id=1, source_target_pairs={{4,0},{0,4},{5,1},{1,5},{6,2},{2,6},{7,3},{3,7},{12,8},{8,12},{13,... | collective-permute-start | bytes 4718600 | tf_op jit(solution)/shard_map/while/body/eval_jaxpr/ppermute | solution.py:36
  425.0 12.1 %copy-start.12 = (f32[1024,768]{1,0:T(8,128)}, f32[1024,768]{1,0:T(8,128)S(1)}, u32[]{:S(2)}) copy-start(f32[1024,768]{1,0:T(8,128)S(1)} %get-tuple-element.111) | copy-start | bytes 9437188
  427.8 10.8 %copy-start.32 = (f32[768,768]{1,0:T(8,128)S(1)}, f32[768,768]{1,0:T(8,128)}, u32[]{:S(2)}) copy-start(f32[768,768]{1,0:T(8,128)} %all-gather.8.cloned.1.call-done) | copy-start | bytes 7077892
  448.5 250.9 %reduce-scatter.15.cloned.1.call-start = ((), (), s32[]{:S(2)}) async-start(), calls=%async_computation.14 | async-start | bytes 884736
  465.1 13.6 %copy-start.21 = (f32[1024,192]{0,1:T(8,128)}, f32[1024,192]{0,1:T(8,128)S(1)}, u32[]{:S(2)}) copy-start(f32[1024,192]{0,1:T(8,128)S(1)} %get-tuple-element.126) | copy-start | bytes 2359300
  517.2 9.4 slice-start.3
  517.2 9.4 slice-start.4
  526.6 10.5 %copy-start.27 = (f32[1024,192]{0,1:T(8,128)S(1)}, f32[1024,192]{0,1:T(8,128)}, u32[]{:S(2)}) copy-start(f32[1024,192]{0,1:T(8,128)} %get-tuple-element.127) | copy-start | bytes 2359300
  537.1 28.4 %slice-start = ((s8[12582912]{0:T(1024)(128)(4,1)}), s8[4194304]{0:T(1024)(128)(4,1)S(1)}, s32[]{:S(2)}) async-start(s8[12582912]{0:T(1024)(128)(4,1)} %bitcast.117), calls=%async_computation.15 | async-start | bytes 8388608
  537.1 28.4 %slice-start.1 = ((s8[12582912]{0:T(1024)(128)(4,1)}), s8[4194304]{0:T(1024)(128)(4,1)S(1)}, s32[]{:S(2)}) async-start(s8[12582912]{0:T(1024)(128)(4,1)} %bitcast.117), calls=%async_computation.16 | async-start | bytes 8388608
  537.1 28.4 %slice-start.2 = ((s8[12582912]{0:T(1024)(128)(4,1)}), s8[4194304]{0:T(1024)(128)(4,1)S(1)}, s32[]{:S(2)}) async-start(s8[12582912]{0:T(1024)(128)(4,1)} %bitcast.117), calls=%async_computation.17 | async-start | bytes 8388608
  553.1 9.5 copy-start
  553.1 9.5 copy-start.34
  564.0 36.2 %collective-permute-start.8 = (f32[1024,384]{0,1:T(8,128)}, f32[1024,384]{0,1:T(8,128)}, u32[]{:S(2)}, u32[]{:S(2)}) collective-permute-start(f32[1024,384]{0,1:T(8,128)} %pad_maximum_fusion.1), channel_id=1, source_target_pairs={{4,0},{0,4},{5,1},{1,5},{6,2},{2,6},{7,3},{3,7},{12,8},{8,12},{13,... | collective-permute-start | bytes 4718600 | tf_op jit(solution)/shard_map/while/body/eval_jaxpr/ppermute | solution.py:36
  578.5 9.6 copy-start.1
  603.3 8.1 copy-start.23
  603.3 38.1 %collective-permute-start.9 = (f32[1024,384]{0,1:T(8,128)}, f32[1024,384]{0,1:T(8,128)S(1)}, u32[]{:S(2)}, u32[]{:S(2)}) collective-permute-start(f32[1024,384]{0,1:T(8,128)} %maximum_add_fusion), channel_id=1, source_target_pairs={{4,0},{0,4},{5,1},{1,5},{6,2},{2,6},{7,3},{3,7},{12,8},{8,12},{13,... | collective-permute-start | bytes 4718600 | tf_op jit(solution)/shard_map/ppermute | solution.py:36
  611.3 15.6 %copy-start.22 = (f32[1024,192]{0,1:T(8,128)S(1)}, f32[1024,192]{0,1:T(8,128)}, u32[]{:S(2)}) copy-start(f32[1024,192]{0,1:T(8,128)} %copy-done.21) | copy-start | bytes 2359300
  611.4 132.5 %all-reduce.12.cloned.1.call-start = ((), (), s32[]{:S(2)}) async-start(), calls=%async_computation.10 | async-start | bytes 6291456 | tf_op jit(solution)/shard_map/psum | solution.py:185
  611.4 15.5 %copy-start.2 = (f32[3,1024,1024]{2,1,0:T(8,128)S(1)}, f32[3,1024,1024]{2,1,0:T(8,128)}, u32[]{:S(2)}) copy-start(f32[3,1024,1024]{2,1,0:T(8,128)} %copy-done.1) | copy-start | bytes 37748740
  658.8 159.1 %reduce-scatter.9.cloned.1.call-start = ((), (), s32[]{:S(2)}) async-start(), calls=%async_computation.11 | async-start | bytes 2654208 | tf_op jit(solution)/shard_map/reduce_scatter | solution.py:189
  672.3 218.3 %reduce-scatter.11.cloned.1.call-start = ((), (), s32[]{:S(2)}) async-start(), calls=%async_computation.12 | async-start | bytes 2654208 | tf_op jit(solution)/shard_map/reduce_scatter | solution.py:190
  672.5 13.1 %copy-start.10 = (f32[1,1024,768]{2,1,0:T(8,128)S(1)}, f32[1,1024,768]{2,1,0:T(8,128)}, u32[]{:S(2)}) copy-start(f32[1,1024,768]{2,1,0:T(8,128)} %param.16) | copy-start | bytes 9437188
  685.5 275.9 %reduce-scatter.13.cloned.1.call-start = ((), (), s32[]{:S(2)}) async-start(), calls=%async_computation.13 | async-start | bytes 2211840
  697.0 46.9 %copy-start.8 = (f32[1024,768]{1,0:T(8,128)S(1)}, f32[1024,768]{1,0:T(8,128)}, u32[]{:S(2)}) copy-start(f32[1024,768]{1,0:T(8,128)} %copy-done.6) | copy-start | bytes 9437188
  (23 other events, 70.7 us)
Sparse Core Ops, SparseCore 0:
  10.2 50.4 all-gather.3
  70.6 54.7 all-gather.5
  198.3 67.7 all-reduce.5
  268.2 51.9 all-gather.7
  349.1 66.9 all-reduce.7
  448.6 68.5 all-reduce.9
  611.5 62.5 reduce-scatter.14
  676.4 67.4 all-reduce.11
  748.0 69.8 reduce-scatter.8
  821.8 68.7 reduce-scatter.10
  894.7 66.7 reduce-scatter.12
